TPU v7x, 512 devices: a whole 4x8x8 slice. The times are simulated.
512 devices in a mesh: ep: 32 (over z, x), fsdp: 16 (over y, core).
Axes of the slice: x: 4, y: 8, z: 8, core: 2. Of those that a mesh axis runs over, the one named last changes fastest.
Arguments:
- train_down: float32 [64, 1408, 2048], P('ep', None, 'fsdp'), may hold values from -0.21875 to 0.21875
- other_down: float32 [64, 1408, 2048], P('ep', None, 'fsdp'), may hold values from -0.15625 to 0.15625
- router_weight: float32 [2048, 64], P('fsdp', 'ep'), may hold values from -0.125 to 0.125
- router_gain: float32 [2048], P('fsdp'), may hold values from 0.25 to 1.75
Outputs:
- ready_down: bfloat16 [64, 1408, 2048], P('ep')
- scale_down: float32 [64, 1408], P('ep')
- serve_router: bfloat16 [2048, 64], replicated
- latest_down: float32 [64, 1408, 2048], P('ep', None, 'fsdp')
All inputs are finite; a program needn't handle non-finite values.
Results may differ from a plain program's by a relative error of at most 0.001.
Values may be sent and summed in bfloat16 or wider, within the bound.
A program may use at most 128 MiB of HBM per device.

v0:
```python
import jax
import jax.numpy as jnp
from jax import lax
from jax.sharding import PartitionSpec as P


def from_everyone(x, axis):
    copies = jnp.broadcast_to(x, (lax.axis_size(axis), *x.shape))
    return lax.all_to_all(copies, axis, split_axis=0, concat_axis=0, tiled=True)


def taken_together(x, axis):
    return from_everyone(x, axis).sum(axis=0)


def laid_out(tiles, dim):
    shape = list(tiles.shape[1:])
    shape[dim] *= tiles.shape[0]
    return jnp.moveaxis(tiles, 0, dim).reshape(shape)


def gathered_copies(x, axis, dim):
    tiles = from_everyone(x, axis)
    return laid_out(tiles, dim)


def on_device(train_down, other_down, router_weight, router_gain):
    latest_down = 0.5 * other_down + 0.5 * train_down
    total_down = taken_together(jnp.sum(latest_down * latest_down, axis=2), "fsdp")
    scale_down = jnp.sqrt(total_down)
    narrow_down = (latest_down / jnp.expand_dims(scale_down, 2)).astype(jnp.bfloat16)
    ready_down = lax.all_gather(narrow_down, "fsdp", axis=2, tiled=True)
    part_router = (router_weight * router_gain[:, None]).astype(jnp.bfloat16)
    row_router = lax.all_gather(part_router, "fsdp", axis=0, tiled=True)
    serve_router = gathered_copies(row_router, "ep", 1)
    return (ready_down, scale_down, serve_router, latest_down)


def solution(mesh):
    placed = (P("ep", None, "fsdp"), P("ep", None, "fsdp"), P("fsdp", "ep"), P("fsdp"))
    return jax.shard_map(
        on_device,
        mesh=mesh,
        in_specs=placed,
        out_specs=(P("ep", None, None), P("ep", None), P(), P("ep", None, "fsdp")),
        check_vma=False,
    )
```

profile of v0, /device:TPU:1, one launch (start us, length us, event | category | flops | bytes accessed | tf_op | source)
XLA Modules:
  0.0 125.7 jit_solution(18168759618692292197)
XLA Ops:
  7.2 0.0 all-gather.2.cloned.1.call-start
  7.2 2.3 %multiply_reduce_fusion = (f32[2,1408]{1,0:T(2,128)S(1)}, f32[2,1408,128]{2,1,0:T(8,128)S(1)}) fusion(f32[2,1408,128]{2,1,0:T(8,128)} %param.5, f32[2,1408,128]{2,1,0:T(8,128)} %param.4), kind=kLoop, calls=%fused_computation.1 | loop fusion | flops 1438976 | bytes 4336640 | tf_op jit(solution)/shard_map/reduce_sum | solution.py:29
  9.5 0.0 copy-start
  9.5 19.2 %all_to_all.10 = f32[16,2,1408]{2,1,0:T(2,128)S(1)} all-to-all(f32[16,2,1408]{2,1,0:T(2,128)S(1)} %broadcast_in_dim.8), channel_id=1, replica_groups=mesh['ep'=32,'fsdp'=16] {'fsdp'}, dimensions={0} | all-to-all | bytes 360448 | tf_op jit(solution)/shard_map/all_to_all | solution.py:9
  28.7 0.1 reduce_sum.19
  28.8 0.0 copy-start.1
  28.8 0.0 copy-start.2
  28.8 0.0 copy-start.3
  28.8 1.3 %divide_convert_fusion = bf16[2,1408,128]{2,1,0:T(8,128)(2,1)} fusion(f32[2,1408,128]{2,1,0:T(8,128)S(1)} %get-tuple-element.13, f32[2,1408]{1,0:T(2,128)S(1)} %sqrt.7), kind=kLoop, calls=%fused_computation | loop fusion | flops 720896 | bytes 2173952 | tf_op jit(solution)/shard_map/convert_element_type | solution.py:31
  30.1 0.0 copy-done
  30.1 0.0 all-gather.2.cloned.1.call-update
  30.2 0.0 copy-done.1
  30.2 0.0 copy-done.2
  30.2 0.0 copy-done.3
  30.2 14.5 %all_gather.7 = bf16[2048,2]{0,1:T(2,128)(2,1)S(1)} all-gather(bf16[128,2]{0,1:T(2,128)(2,1)S(1)} %multiply_convert_fusion), channel_id=1, replica_groups=mesh['ep'=32,'fsdp'=16] {'fsdp'}, dimensions={0}, use_global_device_ids=true | all-gather | bytes 8704 | tf_op jit(solution)/shard_map/all_gather | solution.py:34
  44.7 0.1 broadcast_in_dim.9
  44.8 23.3 %all_to_all.11 = bf16[32,2048,2]{1,2,0:T(2,128)(2,1)S(1)} all-to-all(bf16[32,2048,2]{1,2,0:T(2,128)(2,1)S(1)} %broadcast_in_dim.9), channel_id=1, replica_groups=mesh['ep'=32,'fsdp'=16] {'ep'}, dimensions={0} | all-to-all | bytes 524288 | tf_op jit(solution)/shard_map/all_to_all | solution.py:9
  68.1 0.8 reshape.15
  68.9 39.8 %all-gather.2.cloned.1.call-done = bf16[2,1408,2048]{2,1,0:T(8,128)(2,1)} async-done(((bf16[2,1408,128]{2,1,0:T(8,128)(2,1)}), bf16[2,1408,2048]{2,1,0:T(8,128)(2,1)}) %all-gather.2.cloned.1.call-update) | async-done | bytes 11534352 | tf_op jit(solution)/shard_map/all_gather | solution.py:32
  108.7 10.1 %copy.11 = bf16[2,1408,2048]{2,1,0:T(8,128)(2,1)} copy(bf16[2,1408,2048]{2,1,0:T(8,128)(2,1)} %all-gather.2.cloned.1.call-done) | data formatting | bytes 23068672
  (3 shorter events, 0.1 us)
Async XLA Ops:
  7.2 101.6 %all-gather.2.cloned.1.call-start = ((), (), s32[]{:S(2)}) async-start(), calls=%async_computation.2 | async-start | bytes 12255232 | tf_op jit(solution)/shard_map/all_gather | solution.py:32
  9.5 20.7 %copy-start = (f32[2,1408,128]{2,1,0:T(8,128)}, f32[2,1408,128]{2,1,0:T(8,128)S(1)}, u32[]{:S(2)}) copy-start(f32[2,1408,128]{2,1,0:T(8,128)S(1)} %get-tuple-element.13) | copy-start | bytes 4325380
  28.8 1.4 %copy-start.1 = (f32[2,1408]{1,0:T(2,128)}, f32[2,1408]{1,0:T(2,128)S(1)}, u32[]{:S(2)}) copy-start(f32[2,1408]{1,0:T(2,128)S(1)} %sqrt.7) | copy-start | bytes 33796
  28.8 1.4 %copy-start.2 = (f32[128,2]{0,1:T(2,128)S(1)}, f32[128,2]{0,1:T(2,128)}, u32[]{:S(2)}) copy-start(f32[128,2]{0,1:T(2,128)} %param.6) | copy-start | bytes 3076
  28.8 1.4 %copy-start.3 = (f32[128]{0:T(128)S(1)}, f32[128]{0:T(128)}, u32[]{:S(2)}) copy-start(f32[128]{0:T(128)} %param.7) | copy-start | bytes 1540
Sparse Core Ops, SparseCore 0:
  30.3 78.3 all-gather.1
where the time goes:
time: 126 us
  blocking collectives  57 us (45%)
  waiting for transfers between devices  39.8 us (32%)
  between operations  14.1 us (11%)
  local copies, waits for them, and re-layouts  11.1 us (9%)
  other arithmetic  3.63 us (3%)
    all_to_all x2, blocking collectives, from_everyone(): return lax.all_to_all(copies, axis, split_axis=0, concat_axis=0, tiled=True)  42.5 us
    all_gather x1, waiting for transfers between devices, on_device(): ready_down = lax.all_gather(narrow_down, 'fsdp', axis=2, tiled=True)  39.8 us
    all_gather x1, blocking collectives, on_device(): row_router = lax.all_gather(part_router, 'fsdp', axis=0, tiled=True)  14.5 us
    unnamed x9, local copies, waits for them, and re-layouts  10.1 us
  transfers between devices with their start and end apart: 1, of which 1 were waited for; matrix products, arithmetic and copies ran while one was open for 1% of the time, Pallas kernels for 0%

commit v1 on v0

--- a/solution.py
+++ b/solution.py
@@ -31,7 +31,12 @@
     narrow_down = (latest_down / jnp.expand_dims(scale_down, 2)).astype(jnp.bfloat16)
     ready_down = lax.all_gather(narrow_down, "fsdp", axis=2, tiled=True)
     part_router = (router_weight * router_gain[:, None]).astype(jnp.bfloat16)
-    row_router = lax.all_gather(part_router, "fsdp", axis=0, tiled=True)
+    row_router = jnp.concatenate(
+        jax.lax.all_to_all(
+            jnp.stack([part_router for _ in range(jax.lax.axis_size("fsdp"))], 0), "fsdp", 0, 0
+        ),
+        0,
+    )
     serve_router = gathered_copies(row_router, "ep", 1)
     return (ready_down, scale_down, serve_router, latest_down)
 

time: 126 us -> 126 us (level)
  blocking collectives: 57 us -> 52 us
  waiting for transfers between devices: 39.8 us -> 44.7 us
    all_gather x1 -> x0, blocking collectives: 14.5 us -> none  [on_device(): row_router = lax.all_gather(part_router, 'fsdp', axis=0, tiled=True)]
    all_to_all x0 -> x1, blocking collectives: none -> 9.77 us  [on_device(): jax.lax.all_to_all(jnp.stack([part_router for _ in range(jax.lax.axis_siz...]
    all_gather x1, waiting for transfers between devices: 39.8 us -> 44.7 us  [on_device(): ready_down = lax.all_gather(narrow_down, 'fsdp', axis=2, tiled=True)]
where the time goes in v1:
time: 126 us
  blocking collectives  52 us (41%)
  waiting for transfers between devices  44.7 us (35%)
  between operations  14.1 us (11%)
  local copies, waits for them, and re-layouts  11.1 us (9%)
  other arithmetic  3.63 us (3%)
    all_gather x1, waiting for transfers between devices, on_device(): ready_down = lax.all_gather(narrow_down, 'fsdp', axis=2, tiled=True)  44.7 us
    all_to_all x2, blocking collectives, from_everyone(): return lax.all_to_all(copies, axis, split_axis=0, concat_axis=0, tiled=True)  42.3 us
    unnamed x9, local copies, waits for them, and re-layouts  10.1 us
    all_to_all x1, blocking collectives, on_device(): jax.lax.all_to_all(jnp.stack([part_router for _ in range(jax.lax.axis_siz...  9.77 us
  transfers between devices with their start and end apart: 1, of which 1 were waited for; matrix products, arithmetic and copies ran while one was open for 1% of the time, Pallas kernels for 0%

profile of v1, /device:TPU:1, one launch (start us, length us, event | category | flops | bytes accessed | tf_op | source)
XLA Modules:
  0.0 125.7 jit_solution(15134980987610731615)
XLA Ops:
  7.2 0.0 all-gather.2.cloned.1.call-start
  7.2 2.3 %multiply_reduce_fusion = (f32[2,1408]{1,0:T(2,128)S(1)}, f32[2,1408,128]{2,1,0:T(8,128)S(1)}) fusion(f32[2,1408,128]{2,1,0:T(8,128)} %param.5, f32[2,1408,128]{2,1,0:T(8,128)} %param.4), kind=kLoop, calls=%fused_computation.1 | loop fusion | flops 1438976 | bytes 4336640 | tf_op jit(solution)/shard_map/reduce_sum | solution.py:29
  9.5 0.0 copy-start
  9.5 19.2 %all_to_all.15 = f32[16,2,1408]{2,1,0:T(2,128)S(1)} all-to-all(f32[16,2,1408]{2,1,0:T(2,128)S(1)} %broadcast_in_dim.8), channel_id=1, replica_groups=mesh['ep'=32,'fsdp'=16] {'fsdp'}, dimensions={0} | all-to-all | bytes 360448 | tf_op jit(solution)/shard_map/all_to_all | solution.py:9
  28.7 0.1 reduce_sum.19
  28.8 0.0 copy-start.1
  28.8 0.0 copy-start.2
  28.8 0.0 copy-start.3
  28.8 1.3 %divide_convert_fusion = bf16[2,1408,128]{2,1,0:T(8,128)(2,1)} fusion(f32[2,1408,128]{2,1,0:T(8,128)S(1)} %get-tuple-element.13, f32[2,1408]{1,0:T(2,128)S(1)} %sqrt.7), kind=kLoop, calls=%fused_computation | loop fusion | flops 720896 | bytes 2173952 | tf_op jit(solution)/shard_map/convert_element_type | solution.py:31
  30.1 0.0 copy-done
  30.1 0.0 all-gather.2.cloned.1.call-update
  30.2 0.0 copy-done.1
  30.2 0.0 copy-done.2
  30.2 0.0 copy-done.3
  30.2 9.8 %all_to_all.16 = bf16[16,128,2]{1,2,0:T(2,128)(2,1)S(1)} all-to-all(bf16[16,128,2]{1,2,0:T(2,128)(2,1)S(1)} %stack.2), channel_id=1, replica_groups=mesh['ep'=32,'fsdp'=16] {'fsdp'}, dimensions={0} | all-to-all | bytes 16384 | tf_op jit(solution)/shard_map/all_to_all | solution.py:35
  40.0 0.1 broadcast_in_dim.9
  40.1 23.1 %all_to_all.17 = bf16[32,2048,2]{1,2,0:T(2,128)(2,1)S(1)} all-to-all(bf16[32,2048,2]{1,2,0:T(2,128)(2,1)S(1)} %broadcast_in_dim.9), channel_id=1, replica_groups=mesh['ep'=32,'fsdp'=16] {'ep'}, dimensions={0} | all-to-all | bytes 524288 | tf_op jit(solution)/shard_map/all_to_all | solution.py:9
  63.2 0.8 reshape.21
  64.0 44.7 %all-gather.2.cloned.1.call-done = bf16[2,1408,2048]{2,1,0:T(8,128)(2,1)} async-done(((bf16[2,1408,128]{2,1,0:T(8,128)(2,1)}), bf16[2,1408,2048]{2,1,0:T(8,128)(2,1)}) %all-gather.2.cloned.1.call-update) | async-done | bytes 11534352 | tf_op jit(solution)/shard_map/all_gather | solution.py:32
  108.7 10.1 %copy.11 = bf16[2,1408,2048]{2,1,0:T(8,128)(2,1)} copy(bf16[2,1408,2048]{2,1,0:T(8,128)(2,1)} %all-gather.2.cloned.1.call-done) | data formatting | bytes 23068672
  (4 shorter events, 0.1 us)
Async XLA Ops:
  7.2 101.6 %all-gather.2.cloned.1.call-start = ((), (), s32[]{:S(2)}) async-start(), calls=%async_computation.3 | async-start | bytes 12255232 | tf_op jit(solution)/shard_map/all_gather | solution.py:32
  9.5 20.7 %copy-start = (f32[2,1408,128]{2,1,0:T(8,128)}, f32[2,1408,128]{2,1,0:T(8,128)S(1)}, u32[]{:S(2)}) copy-start(f32[2,1408,128]{2,1,0:T(8,128)S(1)} %get-tuple-element.13) | copy-start | bytes 4325380
  28.8 1.4 %copy-start.1 = (f32[2,1408]{1,0:T(2,128)}, f32[2,1408]{1,0:T(2,128)S(1)}, u32[]{:S(2)}) copy-start(f32[2,1408]{1,0:T(2,128)S(1)} %sqrt.7) | copy-start | bytes 33796
  28.8 1.4 %copy-start.2 = (f32[128,2]{0,1:T(2,128)S(1)}, f32[128,2]{0,1:T(2,128)}, u32[]{:S(2)}) copy-start(f32[128,2]{0,1:T(2,128)} %param.6) | copy-start | bytes 3076
  28.8 1.4 %copy-start.3 = (f32[128]{0:T(128)S(1)}, f32[128]{0:T(128)}, u32[]{:S(2)}) copy-start(f32[128]{0:T(128)} %param.7) | copy-start | bytes 1540
Sparse Core Ops, SparseCore 0:
  30.3 78.3 all-gather.1
